TPU v7x, 8 devices: a whole 2x2x1 slice. The times are simulated.
8 devices in a mesh: data: 1 (over z), cp: 2 (over y), tp: 4 (over x, core).
Axes of the slice: x: 2, y: 2, z: 1, core: 2. Of those that a mesh axis runs over, the one named last changes fastest.
Arguments:
- act_in: bfloat16 [2, 2048, 4096], P(None, ('data', 'cp', 'tp'))
- route_ids: int32 [2, 2048, 2], P(None, ('data', 'cp', 'tp'))
- route_gates: float32 [2, 2048, 2], P(None, ('data', 'cp', 'tp'))
- w_query: bfloat16 [4096, 64, 128], P(None, 'tp')
- w_key: bfloat16 [4096, 4, 128], P(None, 'tp')
- w_value: bfloat16 [4096, 4, 128], P(None, 'tp')
- w_out: bfloat16 [64, 128, 4096], P('tp')
- w_gate: bfloat16 [8, 4096, 1536], P(('cp', 'tp'))
- w_up: bfloat16 [8, 4096, 1536], P(('cp', 'tp'))
- w_down: bfloat16 [8, 1536, 4096], P(('cp', 'tp'))
Outputs:
- output: bfloat16 [2, 2048, 4096], P(None, ('data', 'cp', 'tp'))
All inputs are finite; a program needn't handle non-finite values.
Results may differ from a plain program's by a relative error of at most 0.00591.
Values are sent between devices in bfloat16 or wider.
A program may use at most 1 GiB of HBM per device.

v0:
```python
import jax
import jax.numpy as jnp
from jax import lax
from jax.sharding import PartitionSpec as P


def pick_rows(row_table, row_ids):
    return jnp.take(row_table, row_ids, axis=0, mode='fill', fill_value=0)


def attend_local(act_in, w_query, w_key, w_value, w_out, cp_size, tp_size):
    n_micro, tokens, hidden = act_in.shape
    q_local, head_dim = w_query.shape[1], w_query.shape[2]
    kv_local = w_key.shape[1]
    group_size = q_local // kv_local
    half_rows = tokens * tp_size
    piece_len = half_rows // 2
    seq_len = half_rows * cp_size
    cp_rank = lax.axis_index('cp')
    x_half = lax.all_gather(act_in, 'tp', axis=1, tiled=True)
    query_rows = jnp.einsum('bsh,hnd->bsnd', x_half, w_query, preferred_element_type=jnp.float32).astype(jnp.bfloat16)
    query_rows = query_rows.reshape(n_micro, half_rows, kv_local, group_size, head_dim)
    key_half = jnp.einsum('bsh,hnd->bsnd', x_half, w_key, preferred_element_type=jnp.float32).astype(jnp.bfloat16)
    value_half = jnp.einsum('bsh,hnd->bsnd', x_half, w_value, preferred_element_type=jnp.float32).astype(jnp.bfloat16)
    key_all = lax.all_gather(key_half, 'cp', axis=1, tiled=True)
    value_all = lax.all_gather(value_half, 'cp', axis=1, tiled=True)
    local_ix = jnp.arange(half_rows)
    owner_ix = jnp.arange(cp_size)[:, None]
    key_pos = jnp.where(local_ix < piece_len, owner_ix * piece_len + local_ix, (2 * cp_size - 1 - owner_ix) * piece_len + local_ix - piece_len).reshape(seq_len)
    score_scale = head_dim ** -0.5
    halves = []
    for half_id in range(2):
        piece_id = cp_rank if half_id == 0 else 2 * cp_size - 1 - cp_rank
        query_pos = piece_id * piece_len + jnp.arange(piece_len)
        q_part = query_rows[:, half_id * piece_len:(half_id + 1) * piece_len]
        scores = jnp.einsum('bqhgd,bkhd->bhgqk', q_part, key_all, preferred_element_type=jnp.float32) * score_scale
        scores = jnp.where(key_pos[None, :] <= query_pos[:, None], scores, -jnp.inf)
        row_peak = jnp.max(scores, axis=-1, keepdims=True)
        exp_scores = jnp.exp(scores - row_peak)
        row_sum = jnp.sum(exp_scores, axis=-1)
        weighted = jnp.einsum('bhgqk,bkhd->bqhgd', exp_scores.astype(jnp.bfloat16), value_all, preferred_element_type=jnp.float32)
        weighted = weighted / jnp.transpose(row_sum, (0, 3, 1, 2))[..., None]
        halves.append(weighted.astype(jnp.bfloat16))
    attn_rows = jnp.concatenate(halves, axis=1).reshape(n_micro, half_rows, q_local, head_dim)
    partial = jnp.einsum('bsnd,ndh->bsh', attn_rows, w_out, preferred_element_type=jnp.float32)
    attn_sum = lax.psum_scatter(partial, 'tp', scatter_dimension=1, tiled=True)
    return (act_in.astype(jnp.float32) + attn_sum).astype(jnp.bfloat16)


def dispatch_experts(mid_rows, route_ids, route_gates, w_gate, w_up, w_down, experts):
    n_micro, tokens, hidden = mid_rows.shape
    capacity = (4 * tokens) // experts
    flat_ids = route_ids.reshape(n_micro, 2 * tokens)
    expert_hits = (flat_ids[..., None] == jnp.arange(experts)).astype(jnp.int32)
    slot_rank = jnp.sum((jnp.cumsum(expert_hits, axis=1) - 1) * expert_hits, axis=-1)
    dest_slot = flat_ids * capacity + slot_rank
    micro_ix = jnp.arange(n_micro)[:, None]
    token_of = jnp.broadcast_to((jnp.arange(2 * tokens, dtype=jnp.int32) // 2)[None, :], dest_slot.shape)
    source_row = jnp.full((n_micro, experts * capacity), tokens, jnp.int32).at[micro_ix, dest_slot].set(token_of)
    send_buf = jax.vmap(pick_rows)(mid_rows, source_row).reshape(n_micro, experts, capacity, hidden)
    recv_buf = lax.all_to_all(send_buf, ('cp', 'tp'), 1, 1, tiled=True)
    expert_in = recv_buf.reshape(n_micro, experts * capacity, hidden)
    gate_act = jnp.einsum('bth,hf->btf', expert_in, w_gate[0], preferred_element_type=jnp.float32)
    up_act = jnp.einsum('bth,hf->btf', expert_in, w_up[0], preferred_element_type=jnp.float32)
    mixed_act = (jax.nn.silu(gate_act) * up_act).astype(jnp.bfloat16)
    expert_out = jnp.einsum('btf,fh->bth', mixed_act, w_down[0], preferred_element_type=jnp.float32).astype(jnp.bfloat16)
    back_buf = lax.all_to_all(expert_out.reshape(n_micro, experts, capacity, hidden), ('cp', 'tp'), 1, 1, tiled=True)
    picked = jax.vmap(pick_rows)(back_buf.reshape(n_micro, experts * capacity, hidden), dest_slot).reshape(n_micro, tokens, 2, hidden)
    combined = route_gates[:, :, 0:1] * picked[:, :, 0].astype(jnp.float32) + route_gates[:, :, 1:2] * picked[:, :, 1].astype(jnp.float32)
    return (mid_rows.astype(jnp.float32) + combined).astype(jnp.bfloat16)


def solution(mesh):
    cp_size = mesh.shape['cp']
    tp_size = mesh.shape['tp']
    experts = cp_size * tp_size
    row_spec = P(None, ('data', 'cp', 'tp'), None)
    head_spec = P(None, 'tp', None)
    out_spec = P('tp', None, None)
    expert_spec = P(('cp', 'tp'), None, None)

    def device_step(act_in, route_ids, route_gates, w_query, w_key, w_value, w_out, w_gate, w_up, w_down):
        mid_rows = attend_local(act_in, w_query, w_key, w_value, w_out, cp_size, tp_size)
        return dispatch_experts(mid_rows, route_ids, route_gates, w_gate, w_up, w_down, experts)

    return jax.shard_map(device_step, mesh=mesh, in_specs=(row_spec, row_spec, row_spec, head_spec, head_spec, head_spec, out_spec, expert_spec, expert_spec, expert_spec), out_specs=row_spec, check_vma=False)
```

profile of v0, /device:TPU:0, one launch (start us, length us, event | category | flops | bytes accessed | tf_op | source)
XLA Modules:
  0.0 1432.6 jit_solution(11077063319769445920)
XLA Ops:
  9.6 106.4 %all-gather.6.cloned.1.call-done = bf16[2,1024,4096]{2,1,0:T(8,128)(2,1)} async-done(((bf16[2,256,4096]{2,1,0:T(8,128)(2,1)}), bf16[2,1024,4096]{2,1,0:T(8,128)(2,1)}) %all-gather.6.cloned.1.call-update) | async-done | bytes 16777232 | tf_op jit(solution)/shard_map/all_gather | solution.py:20
  115.9 9.0 convolution_convert_fusion
  125.0 9.0 convolution_convert_fusion.1
  134.5 42.7 %convert_bitcast_fusion = bf16[2,1024,1,16,128]{4,1,3,0,2:T(8,128)(2,1)} fusion(bf16[4096,16,128]{2,1,0:T(8,128)(2,1)} %param.13, bf16[2,1024,4096]{2,1,0:T(8,128)(2,1)} %all-gather.6.cloned.1.call-done), kind=kOutput, calls=%fused_computation.49 | convolution fusion | flops 34363932672 | bytes 41943040 | tf_op jit(solution)/shard_map/bsh,hnd->bsnd/dot_general | solution.py:21
  177.2 47.2 %fusion.4 = (f32[2,16,512]{2,1,0:T(8,128)S(1)}, f32[2,2048,512,16]{2,1,3,0:T(8,128)}) fusion(pred[512,2048]{0,1:T(8,128)(4,1)S(1)} %get-tuple-element.7, bf16[2,1024,1,16,128]{4,1,3,0,2:T(8,128)(2,1)} %convert_bitcast_fusion, bf16[2,2048,128]{2,1,0:T(8,128)(2,1)} %all-gather.10.cloned.1.call-done), kind=kOutput, calls=%fused_computation.11 | convolution fusion | flops 8690581504 | bytes 140574720 | tf_op jit(solution)/shard_map/bqhgd,bkhd->bhgqk/dot_general | solution.py:36
  224.4 41.3 %fusion = f32[2,16,512]{2,1,0:T(8,128)S(1)} fusion(f32[2,2048,512,16]{2,1,3,0:T(8,128)} %get-tuple-element.14, f32[2,16,512]{2,1,0:T(8,128)S(1)} %get-tuple-element.13, pred[512,2048]{0,1:T(8,128)(4,1)S(1)} %get-tuple-element.7), kind=kLoop, calls=%fused_computation.7 | loop fusion | flops 134201344 | bytes 135397376 | tf_op jit(solution)/shard_map/reduce_sum | solution.py:40
  265.7 46.9 %fusion.5 = (f32[2,16,512]{2,1,0:T(8,128)S(1)}, f32[2,2048,512,16]{2,1,3,0:T(8,128)}) fusion(pred[512,2048]{0,1:T(8,128)(4,1)S(1)} %copy-done.3, bf16[2,1024,1,16,128]{4,1,3,0,2:T(8,128)(2,1)} %convert_bitcast_fusion, bf16[2,2048,128]{2,1,0:T(8,128)(2,1)S(1)} %copy-done.14), kind=kOutput, calls=%fused_computation.12 | convolution fusion | flops 8690581504 | bytes 140574720 | tf_op jit(solution)/shard_map/bqhgd,bkhd->bhgqk/dot_general | solution.py:36
  312.5 41.1 %fusion.2 = f32[2,16,512]{2,1,0:T(8,128)S(1)} fusion(f32[2,2048,512,16]{2,1,3,0:T(8,128)} %get-tuple-element.12, f32[2,16,512]{2,1,0:T(8,128)S(1)} %get-tuple-element.11, pred[512,2048]{0,1:T(8,128)(4,1)S(1)} %copy-done.3), kind=kLoop, calls=%fused_computation.9 | loop fusion | flops 134201344 | bytes 135397376 | tf_op jit(solution)/shard_map/reduce_sum | solution.py:40
  353.7 48.3 %fusion.38 = bf16[2,512,1,16,128]{1,4,3,0,2:T(8,128)(2,1)} fusion(f32[2,512,16]{1,2,0:T(8,128)S(1)} %bitcast.217, f32[2,2048,512,16]{2,1,3,0:T(8,128)} %get-tuple-element.14, f32[2,16,512]{2,1,0:T(8,128)S(1)} %get-tuple-element.13, pred[512,2048]{0,1:T(8,128)(4,1)S(1)} %get-tuple-element.7, bf16[2,2048,128]{2,1,0:T(8,128)(2,1)} %all-gather.8.cloned.1.call-done), kind=kOutput, calls=%fused_computation.46 | convolution fusion | flops 8728346624 | bytes 140640256 | tf_op jit(solution)/shard_map/bhgqk,bkhd->bqhgd/dot_general | solution.py:41
  402.0 47.6 %fusion.37 = bf16[2,512,1,16,128]{1,4,3,0,2:T(8,128)(2,1)} fusion(f32[2,512,16]{1,2,0:T(8,128)S(1)} %bitcast.218, f32[2,2048,512,16]{2,1,3,0:T(8,128)} %get-tuple-element.12, f32[2,16,512]{2,1,0:T(8,128)S(1)} %get-tuple-element.11, pred[512,2048]{0,1:T(8,128)(4,1)S(1)} %copy-done.3, bf16[2,2048,128]{2,1,0:T(8,128)(2,1)S(1)} %copy-done.13), kind=kOutput, calls=%fused_computation.44 | convolution fusion | flops 8728346624 | bytes 140640256 | tf_op jit(solution)/shard_map/bhgqk,bkhd->bqhgd/dot_general | solution.py:41
  449.6 44.2 %fusion.20 = f32[2,1024,4096]{2,1,0:T(8,128)} fusion(bf16[16,128,4096]{2,1,0:T(8,128)(2,1)} %param.16, bf16[2,512,1,16,128]{1,4,3,0,2:T(8,128)(2,1)} %fusion.37, bf16[2,512,1,16,128]{1,4,3,0,2:T(8,128)(2,1)} %fusion.38), kind=kOutput, calls=%fused_computation.26 | convolution fusion | flops 34376515584 | bytes 58720256 | tf_op jit(solution)/shard_map/bsnd,ndh->bsh/dot_general | solution.py:45
  503.5 216.5 %reduce-scatter.2.cloned.1.call-done = f32[2,256,4096]{2,1,0:T(8,128)} async-done(((f32[2,1024,4096]{2,1,0:T(8,128)}), f32[2,256,4096]{2,1,0:T(8,128)}) %reduce-scatter.2.cloned.1.call-update) | async-done | bytes 8388624 | tf_op jit(solution)/shard_map/reduce_scatter | solution.py:46
  720.0 8.0 add_convert_fusion
  728.0 115.5 %gather_fusion = bf16[2048,4096]{1,0:T(8,128)(2,1)} fusion(bf16[2,256,4096]{2,1,0:T(8,128)(2,1)} %add_convert_fusion, s32[2048]{0:T(1024)S(1)} %bitcast.211), kind=kCustom, calls=%fused_computation | custom fusion | bytes 33570816 | tf_op jit(solution)/shard_map/vmap(jit(_take))/gather | solution.py:8
  843.5 8.3 copy_select_fusion
  851.8 185.4 %all_to_all.10 = bf16[2,8,128,4096]{3,2,0,1:T(8,128)(2,1)S(1)} all-to-all(bf16[2,8,128,4096]{3,2,0,1:T(8,128)(2,1)S(1)} %copy_select_fusion), channel_id=1, replica_groups=mesh['data'=1,'cp'=2,'tp'=4] {'cp','tp'}, dimensions={1} | all-to-all | bytes 33554432 | tf_op jit(solution)/shard_map/all_to_all | solution.py:61
  1043.7 34.2 %fusion.27 = f32[2,1024,1536]{2,1,0:T(8,128)} fusion(bf16[2,1024,4096]{2,1,0:T(8,128)(2,1)} %bitcast.214, bf16[1,4096,1536]{2,1,0:T(8,128)(2,1)} %param.17), kind=kOutput, calls=%fused_computation.31 | convolution fusion | flops 25769803776 | bytes 41943040 | tf_op jit(solution)/shard_map/bth,hf->btf/dot_general | solution.py:63
  1078.0 35.1 %multiply_convert_fusion = bf16[2,1024,1536]{2,1,0:T(8,128)(2,1)} fusion(f32[2,1024,1536]{2,1,0:T(8,128)} %fusion.27, bf16[2,1024,4096]{2,1,0:T(8,128)(2,1)S(1)} %bitcast.215, bf16[1,4096,1536]{2,1,0:T(8,128)(2,1)} %param.18), kind=kOutput, calls=%fused_computation.33 | convolution fusion | flops 25788678144 | bytes 48234496 | tf_op jit(solution)/shard_map/bth,hf->btf/dot_general | solution.py:64
  1113.1 30.8 %fusion.29 = bf16[2,1024,4096]{2,1,0:T(8,128)(2,1)S(1)} fusion(bf16[2,1024,1536]{2,1,0:T(8,128)(2,1)} %multiply_convert_fusion, bf16[1,1536,4096]{2,1,0:T(8,128)(2,1)} %param.19), kind=kOutput, calls=%fused_computation.34 | convolution fusion | flops 25778192384 | bytes 35651584 | tf_op jit(solution)/shard_map/btf,fh->bth/dot_general | solution.py:66
  1155.6 183.5 %all-to-all-done.1 = bf16[2,8,128,4096]{3,2,0,1:T(8,128)(2,1)} async-done(((bf16[2,8,128,4096]{3,2,0,1:T(8,128)(2,1)}), bf16[2,8,128,4096]{3,2,0,1:T(8,128)(2,1)}, u32[]{:S(2)}, u32[]{:S(2)}) %all-to-all-start.1) | async-done | bytes 16777248 | tf_op jit(solution)/shard_map/all_to_all | solution.py:67
  1339.1 14.0 copy.58
  1353.1 34.2 %gather_fusion.1 = bf16[1024,4096]{1,0:T(8,128)(2,1)} fusion(bf16[2,1024,4096]{2,1,0:T(8,128)(2,1)} %bitcast.210, s32[1024]{0:T(1024)S(1)} %bitcast.212), kind=kCustom, calls=%fused_computation.1 | custom fusion | bytes 16785408 | tf_op jit(solution)/shard_map/vmap(jit(_take))/gather | solution.py:8
  1387.3 14.5 %gather.15 = bf16[2,256,2,4096]{3,2,1,0:T(2,128)(2,1)} reshape(bf16[1024,4096]{1,0:T(8,128)(2,1)} %gather_fusion.1) | data formatting | bytes 16777216 | tf_op jit(solution)/shard_map/vmap(jit(_take))/gather | solution.py:8
  1401.8 16.3 %copy_select_fusion.1 = bf16[2,256,2,4096]{3,1,0,2:T(8,128)(2,1)} fusion(bf16[2,256,2,4096]{3,2,1,0:T(2,128)(2,1)} %gather.15, pred[2,256,2]{1,0,2:T(4,128)(4,1)S(1)} %copy.53), kind=kLoop, calls=%fused_computation.47 | loop fusion | flops 4194304 | bytes 16778240 | tf_op jit(solution)/shard_map/vmap(jit(_take))/select_n | solution.py:8
  (83 shorter events, 38.6 us)
Async XLA Ops:
  6.5 109.4 %copy-start = (bf16[4096,1,128]{2,0,1:T(8,128)(2,1)S(1)}, bf16[4096,1,128]{2,0,1:T(8,128)(2,1)}, u32[]{:S(2)}) copy-start(bf16[4096,1,128]{2,0,1:T(8,128)(2,1)} %param.14) | copy-start | bytes 3145732
  6.5 118.4 %copy-start.12 = (bf16[4096,1,128]{2,0,1:T(8,128)(2,1)S(1)}, bf16[4096,1,128]{2,0,1:T(8,128)(2,1)}, u32[]{:S(2)}) copy-start(bf16[4096,1,128]{2,0,1:T(8,128)(2,1)} %param.15) | copy-start | bytes 3145732
  6.5 109.4 %all-gather.6.cloned.1.call-start = ((), (), s32[]{:S(2)}) async-start(), calls=%async_computation.3 | async-start | bytes 20971520 | tf_op jit(solution)/shard_map/all_gather | solution.py:20
  7.3 169.9 %all-gather.10.cloned.1.call-start = ((), (), s32[]{:S(2)}) async-start(), calls=%async_computation.6 | async-start | bytes 1572864 | tf_op jit(solution)/shard_map/all_gather | solution.py:25
  124.9 228.7 %all-gather.8.cloned.1.call-start = ((), (), s32[]{:S(2)}) async-start(), calls=%async_computation.5 | async-start | bytes 1572864 | tf_op jit(solution)/shard_map/all_gather | solution.py:26
  133.9 586.1 %reduce-scatter.2.cloned.1.call-start = ((), (), s32[]{:S(2)}) async-start(), calls=%async_computation.4 | async-start | bytes 41943040 | tf_op jit(solution)/shard_map/reduce_scatter | solution.py:46
  224.4 41.3 %copy-start.3 = (pred[512,2048]{0,1:T(8,128)(4,1)S(1)}, pred[512,2048]{0,1:T(8,128)(4,1)}, u32[]{:S(2)}) copy-start(pred[512,2048]{0,1:T(8,128)(4,1)} %get-tuple-element.8) | copy-start | bytes 3145732
  224.4 41.3 %copy-start.14 = (bf16[2,2048,128]{2,1,0:T(8,128)(2,1)S(1)}, bf16[2,2048,128]{2,1,0:T(8,128)(2,1)}, u32[]{:S(2)}) copy-start(bf16[2,2048,128]{2,1,0:T(8,128)(2,1)} %all-gather.10.cloned.1.call-done) | copy-start | bytes 3145732
  353.6 48.3 %copy-start.13 = (bf16[2,2048,128]{2,1,0:T(8,128)(2,1)S(1)}, bf16[2,2048,128]{2,1,0:T(8,128)(2,1)}, u32[]{:S(2)}) copy-start(bf16[2,2048,128]{2,1,0:T(8,128)(2,1)} %all-gather.8.cloned.1.call-done) | copy-start | bytes 3145732
  493.8 0.7 copy-start.4
  493.8 4.9 copy-start.10
  493.8 5.0 copy-start.11
  498.1 345.4 %copy-start.6 = (s32[2,512]{1,0:T(2,128)}, s32[2,512]{1,0:T(2,128)S(1)}, u32[]{:S(2)}) copy-start(s32[2,512]{1,0:T(2,128)S(1)} %fusion.57) | copy-start | bytes 12292
  1043.7 34.2 %copy-start.2 = (bf16[2,8,128,4096]{3,2,1,0:T(8,128)(2,1)S(1)}, bf16[2,8,128,4096]{3,2,1,0:T(8,128)(2,1)}, u32[]{:S(2)}) copy-start(bf16[2,8,128,4096]{3,2,1,0:T(8,128)(2,1)} %copy.56) | copy-start | bytes 50331652
  1150.5 4.6 copy-start.7
  1150.5 4.9 copy-start.8
  1150.5 5.0 copy-start.5
  1150.5 5.0 copy-start.9
  1150.5 188.6 %all-to-all-start.1 = ((bf16[2,8,128,4096]{3,2,0,1:T(8,128)(2,1)}), bf16[2,8,128,4096]{3,2,0,1:T(8,128)(2,1)}, u32[]{:S(2)}, u32[]{:S(2)}) async-start(bf16[2,8,128,4096]{3,2,0,1:T(8,128)(2,1)} %copy.57), calls=%async_computation.2 | async-start | bytes 33554432 | tf_op jit(solution)/shard_map/all_to_all | solution.py:67
  1387.3 38.3 %copy-start.1 = (bf16[4096,1,128]{2,0,1:T(8,128)(2,1)S(1)}, bf16[4096,1,128]{2,0,1:T(8,128)(2,1)}, u32[]{:S(2)}) copy-start(bf16[4096,1,128]{2,0,1:T(8,128)(2,1)} %param.14) | copy-start | bytes 3145732
Sparse Core Ops, SparseCore 0:
  8.9 107.0 all-gather.5
  125.0 18.2 all-gather.9
  144.8 18.2 all-gather.7
  494.0 225.9 reduce-scatter.1
where the time goes:
time: 1440 us; the launch traced here: 1430 us
  waiting for transfers between devices  507 us (35%)
  matrix products  395 us (27%)
  local copies, waits for them, and re-layouts  198 us (14%)
  blocking collectives  185 us (13%)
  other arithmetic  128 us (9%)
    reduce_scatter x1, waiting for transfers between devices, attend_local(): attn_sum = lax.psum_scatter(partial, 'tp', scatter_dimension=1, tiled=True)  217 us
    all_to_all x1, blocking collectives, dispatch_experts(): recv_buf = lax.all_to_all(send_buf, ('cp', 'tp'), 1, 1, tiled=True)  185 us
    all_to_all x1, waiting for transfers between devices, dispatch_experts(): lax.all_to_all(expert_out.reshape(n_micro, experts, capacity, hidden), ('...  184 us
    gather x3, local copies, waits for them, and re-layouts, pick_rows(): return jnp.take(row_table, row_ids, axis=0, mode='fill', fill_value=0)  164 us
    all_gather x1, waiting for transfers between devices, attend_local(): x_half = lax.all_gather(act_in, 'tp', axis=1, tiled=True)  106 us
    dot_general x2, matrix products, attend_local(): jnp.einsum('bhgqk,bkhd->bqhgd', exp_scores.astype(jnp.bfloat16), value_al...  96 us
    dot_general x2, matrix products, attend_local(): jnp.einsum('bqhgd,bkhd->bhgqk', q_part, key_all, preferred_element_type=j...  94 us
    reduce_sum x2, other arithmetic, attend_local(): row_sum = jnp.sum(exp_scores, axis=-1)  82.4 us
  transfers between devices with their start and end apart: 5, of which 3 were waited for; matrix products, arithmetic and copies ran while one was open for 17% of the time, Pallas kernels for 0%

commit v1 on v0

v1 whole, which is shorter than its diff:
```python
import functools
import math
import jax
import jax.numpy as jnp
from jax import lax
from jax.experimental import pallas as pl
from jax.experimental.pallas import tpu as pltpu
from jax.sharding import PartitionSpec as P

F32 = jnp.float32
BF16 = jnp.bfloat16


def attend_kernel(cp_ref, q_ref, own_ref, other_ref, o_ref, kt_own, kt_other, *, piece, head_dim):
    tile = piece // 2
    exp_scale = (head_dim ** -0.5) * math.log2(math.e)

    @pl.when(pl.program_id(0) == 0)
    def _():
        kt_own[...] = own_ref[:, :head_dim].T
        kt_other[...] = other_ref[:, :head_dim].T

    row_ix = lax.broadcasted_iota(jnp.int32, (tile, tile), 0)
    col_ix = lax.broadcasted_iota(jnp.int32, (tile, tile), 1)

    def one_tile(q_start, full_parts, diag_start):
        q_rows = q_ref[q_start:q_start + tile, :]
        scores, values = [], []
        for k_t, kv, start, size in full_parts:
            scores.append(jnp.dot(q_rows, k_t[:, start:start + size], preferred_element_type=F32))
            values.append((kv, start, size))
        diag = jnp.dot(q_rows, kt_own[:, diag_start:diag_start + tile], preferred_element_type=F32)
        scores.append(jnp.where(col_ix <= row_ix, diag, -jnp.inf))
        values.append((own_ref, diag_start, tile))
        peak = jnp.max(scores[0], axis=-1, keepdims=True)
        for part in scores[1:]:
            peak = jnp.maximum(peak, jnp.max(part, axis=-1, keepdims=True))
        peak = peak * exp_scale
        total = jnp.zeros((tile, 1), F32)
        acc = jnp.zeros((tile, head_dim), F32)
        for part, (kv, start, size) in zip(scores, values):
            weights = jnp.exp2(part * exp_scale - peak)
            total = total + jnp.sum(weights, axis=-1, keepdims=True)
            acc = acc + jnp.dot(weights.astype(BF16), kv[start:start + size, head_dim:], preferred_element_type=F32)
        o_ref[q_start:q_start + tile, :] = (acc / total).astype(BF16)

    def piece_tiles(q_start, full_parts):
        one_tile(q_start, full_parts, q_start)
        one_tile(q_start + tile, full_parts + [(kt_own, own_ref, q_start, tile)], q_start + tile)

    own_low = (kt_own, own_ref, 0, piece)
    other_low = (kt_other, other_ref, 0, piece)
    other_high = (kt_other, other_ref, piece, piece)

    @pl.when(cp_ref[0] == 0)
    def _():
        piece_tiles(0, [])
        piece_tiles(piece, [own_low, other_low, other_high])

    @pl.when(cp_ref[0] == 1)
    def _():
        piece_tiles(0, [other_low])
        piece_tiles(piece, [own_low, other_low])


def attend(q_rows, kv_own, kv_other, cp_rank, head_dim):
    rows, width = q_rows.shape
    heads = width // head_dim
    piece = rows // 2
    kv_spec = pl.BlockSpec((rows, 2 * head_dim), lambda h, s: (0, 0))
    head_spec = pl.BlockSpec((rows, head_dim), lambda h, s: (0, h))
    work = 5 * piece * piece * heads
    return pl.pallas_call(
        functools.partial(attend_kernel, piece=piece, head_dim=head_dim),
        out_shape=jax.ShapeDtypeStruct((rows, width), BF16),
        grid_spec=pltpu.PrefetchScalarGridSpec(
            num_scalar_prefetch=1,
            grid=(heads,),
            in_specs=[head_spec, kv_spec, kv_spec],
            out_specs=head_spec,
            scratch_shapes=[pltpu.VMEM((head_dim, rows), BF16), pltpu.VMEM((head_dim, rows), BF16)],
        ),
        compiler_params=pltpu.CompilerParams(dimension_semantics=('arbitrary',)),
        cost_estimate=pl.CostEstimate(flops=4 * work * head_dim * 2, bytes_accessed=4 * rows * width + 8 * rows * head_dim, transcendentals=work),
        name='attend',
    )(cp_rank.reshape(1), q_rows, kv_own, kv_other)


def rank_in_expert(token_hits):
    tokens = token_hits.shape[-2]
    earlier = (jnp.arange(tokens)[None, :] < jnp.arange(tokens)[:, None]).astype(BF16)
    return jnp.einsum('ts,...se->...te', earlier, token_hits.astype(BF16), preferred_element_type=F32).astype(jnp.int32)


def solution(mesh):
    cp_size = mesh.shape['cp']
    tp_size = mesh.shape['tp']
    experts = cp_size * tp_size
    row_spec = P(None, ('data', 'cp', 'tp'), None)
    head_spec = P(None, 'tp', None)
    out_spec = P('tp', None, None)
    expert_spec = P(('cp', 'tp'), None, None)
    both = ('cp', 'tp')

    def device_step(act_in, route_ids, route_gates, w_query, w_key, w_value, w_out, w_gate, w_up, w_down):
        n_seq, tokens, hidden = act_in.shape
        head_dim = w_query.shape[2]
        capacity = (4 * tokens) // experts
        cp_rank = lax.axis_index('cp')
        my_expert = cp_rank * tp_size + lax.axis_index('tp')
        w_q = w_query.reshape(hidden, -1)
        w_kv = jnp.concatenate([w_key.reshape(hidden, -1), w_value.reshape(hidden, -1)], axis=1)
        w_o = w_out.reshape(-1, hidden)

        ids_all = lax.all_gather(route_ids, both, axis=0)
        hit_here = jnp.any(ids_all == my_expert, axis=-1)
        rank_here = rank_in_expert(hit_here[..., None])[..., 0]
        slot_token = jnp.where(hit_here, rank_here, -1)[:, :, None, :] == jnp.arange(capacity)[:, None]
        pick_in = slot_token.astype(BF16)

        hits = route_ids[..., None] == jnp.arange(experts)
        ranks = rank_in_expert(jnp.any(hits, axis=2))
        choice_rank = jnp.sum(hits * ranks[:, :, None, :], axis=-1)
        choice_slot = route_ids * capacity + choice_rank
        choice_slot = jnp.swapaxes(choice_slot, 1, 2).reshape(n_seq, 2 * tokens)
        pick_back = (choice_slot[..., None] == jnp.arange(experts * capacity)).astype(BF16)

        swap = [(i, i ^ 1) for i in range(cp_size)]
        outs = []
        for seq in range(n_seq):
            x_own = act_in[seq]
            x_half = lax.all_gather(x_own, 'tp', axis=0, tiled=True)
            if seq == 0:
                x_half, pick_in, pick_back = lax.optimization_barrier((x_half, pick_in, pick_back))
            kv_own = jnp.dot(x_half, w_kv, preferred_element_type=F32).astype(BF16)
            kv_other = lax.ppermute(kv_own, 'cp', swap)
            q_rows = jnp.dot(x_half, w_q, preferred_element_type=F32).astype(BF16)
            attn_rows = attend(q_rows, kv_own, kv_other, cp_rank, head_dim)
            partial = jnp.dot(attn_rows, w_o, preferred_element_type=F32)
            attn_sum = lax.psum_scatter(partial, 'tp', scatter_dimension=0, tiled=True)
            if seq > 0:
                x_own, mid_rows = lax.optimization_barrier((x_own, mid_rows))
            mid_rows = (x_own.astype(F32) + attn_sum).astype(BF16)
            mid_all = lax.all_gather(mid_rows, both, axis=0)
            expert_in = jnp.einsum('dst,dth->dsh', pick_in[:, seq], mid_all, preferred_element_type=F32).astype(BF16)
            expert_in = expert_in.reshape(experts * capacity, hidden)
            gate_act = jnp.dot(expert_in, w_gate[0], preferred_element_type=F32)
            up_act = jnp.dot(expert_in, w_up[0], preferred_element_type=F32)
            mixed_act = (jax.nn.silu(gate_act) * up_act).astype(BF16)
            expert_out = jnp.dot(mixed_act, w_down[0], preferred_element_type=F32).astype(BF16)
            back = lax.all_to_all(expert_out.reshape(experts, capacity, hidden), both, 0, 0, tiled=True)
            back = back.reshape(experts * capacity, hidden)
            picked = jnp.dot(pick_back[seq], back, preferred_element_type=F32).astype(BF16)
            combined = route_gates[seq, :, 0:1] * picked[:tokens].astype(F32) + route_gates[seq, :, 1:2] * picked[tokens:].astype(F32)
            outs.append((mid_rows.astype(F32) + combined).astype(BF16))
        return jnp.stack(outs)

    return jax.shard_map(device_step, mesh=mesh, in_specs=(row_spec, row_spec, row_spec, head_spec, head_spec, head_spec, out_spec, expert_spec, expert_spec, expert_spec), out_specs=row_spec, check_vma=False)
```

time: 1440 us -> 799 us (0.55)
  local copies, waits for them, and re-layouts: 198 us -> 7.18 us
  blocking collectives: 185 us -> 14.3 us
  matrix products: 395 us -> 255 us
  waiting for transfers between devices: 507 us -> 388 us
  other arithmetic: 128 us -> 17.7 us
  Pallas kernels: 0 us -> 82.2 us
    all_to_all x1 -> x0, blocking collectives: 185 us -> none  [dispatch_experts(): recv_buf = lax.all_to_all(send_buf, ('cp', 'tp'), 1, 1, tiled=True)]
    gather x3 -> x0, local copies, waits for them, and re-layouts: 164 us -> none  [pick_rows(): return jnp.take(row_table, row_ids, axis=0, mode='fill', fill_value=0)]
    dot_general x11 -> x18, matrix products: 395 us -> 255 us  [the longest x2 47.2 us: device_step(): partial = jnp.dot(attn_rows, w_o, preferred_element_type=F32)]
    all_to_all x1 -> x2, waiting for transfers between devices: 184 us -> 98.4 us  [device_step(): lax.all_to_all(expert_out.reshape(experts, capacity, hidden), both, 0, 0,...]
    reduce_sum x3 -> x1, other arithmetic: 82.5 us -> 0.05 us  [device_step(): choice_rank = jnp.sum(hits * ranks[:, :, None, :], axis=-1)]
    pallas_call x0 -> x2, Pallas kernels: none -> 82.2 us  [attend(): pl.pallas_call(functools.partial(attend_kernel, piece=piece, head_dim=hea...]
    reduce_scatter x1 -> x2, waiting for transfers between devices: 217 us -> 140 us  [device_step(): attn_sum = lax.psum_scatter(partial, 'tp', scatter_dimension=0, tiled=True)]
    all_gather x3 -> x4, waiting for transfers between devices: 106 us -> 149 us  [the longest x2 109 us: device_step(): mid_all = lax.all_gather(mid_rows, both, axis=0)]
  transfers between devices with their start and end apart: 5 -> 10, of which waited for: 3 -> 7; matrix products, arithmetic and copies ran while one was open for 17% -> 32% of each run, Pallas kernels for 0% -> 10%
where the time goes in v1:
time: 799 us; the launch traced here: 796 us
  waiting for transfers between devices  388 us (49%)
  matrix products  255 us (32%)
  Pallas kernels  82.2 us (10%)
  other arithmetic  17.7 us (2%)
  starting transfers between devices  17.2 us (2%)
  blocking collectives  14.3 us (2%)
  between operations  14 us (2%)
    reduce_scatter x2, waiting for transfers between devices, device_step(): attn_sum = lax.psum_scatter(partial, 'tp', scatter_dimension=0, tiled=True)  140 us
    all_gather x2, waiting for transfers between devices, device_step(): mid_all = lax.all_gather(mid_rows, both, axis=0)  109 us
    all_to_all x2, waiting for transfers between devices, device_step(): lax.all_to_all(expert_out.reshape(experts, capacity, hidden), both, 0, 0,...  98.4 us
    pallas_call x2, Pallas kernels, attend(): pl.pallas_call(functools.partial(attend_kernel, piece=piece, head_dim=hea...  82.2 us
    dot_general x2, matrix products, device_step(): partial = jnp.dot(attn_rows, w_o, preferred_element_type=F32)  47.2 us
    dot_general x2, matrix products, device_step(): q_rows = jnp.dot(x_half, w_q, preferred_element_type=F32).astype(BF16)  45.3 us
    dot_general x2, matrix products, device_step(): up_act = jnp.dot(expert_in, w_up[0], preferred_element_type=F32)  40.7 us
    all_gather x2, waiting for transfers between devices, device_step(): x_half = lax.all_gather(x_own, 'tp', axis=0, tiled=True)  40.1 us
  transfers between devices with their start and end apart: 10, of which 7 were waited for; matrix products, arithmetic and copies ran while one was open for 32% of the time, Pallas kernels for 10%

profile of v1, /device:TPU:0, one launch (start us, length us, event | category | flops | bytes accessed | tf_op | source)
XLA Modules:
  0.0 795.9 jit_solution(11547063291901772236)
XLA Ops:
  12.8 14.3 %all-gather.1 = s32[16,256,2]{1,2,0:T(2,128)S(1)} all-gather(s32[2,256,2]{1,2,0:T(2,128)S(1)} %copy-done.8), channel_id=3, replica_groups=mesh['data'=1,'cp'=2,'tp'=4] {'cp','tp'}, dimensions={0}, use_global_device_ids=true | all-gather | bytes 36864 | tf_op jit(solution)/shard_map/all_gather | solution.py:115
  30.7 40.1 %all-gather.10.cloned.1.call-done = bf16[1,1024,4096]{2,1,0:T(8,128)(2,1)} async-done(((bf16[1,256,4096]{2,1,0:T(8,128)(2,1)}), bf16[1,1024,4096]{2,1,0:T(8,128)(2,1)}) %all-gather.10.cloned.1.call-update) | async-done | bytes 8388624 | tf_op jit(solution)/shard_map/all_gather | solution.py:132
  78.2 22.9 %fusion.33.q_ref = bf16[1024,2048]{1,0:T(8,128)(2,1)} fusion(bf16[1024,4096]{1,0:T(8,128)(2,1)S(1)} %bitcast.133, bf16[512,8,16,128]{3,2,1,0:T(8,128)(2,1)} %bitcast.124), kind=kOutput, calls=%fused_computation.37 | convolution fusion | flops 17181966336 | bytes 29360128 | tf_op jit(solution)/shard_map/dot_general | solution.py:137
  101.9 41.1 %attend.2 = bf16[1024,2048]{1,0:T(8,128)(2,1)} custom-call(s32[1]{0:T(128)} %bitcast.1.cp_ref, bf16[1024,2048]{1,0:T(8,128)(2,1)} %fusion.33.q_ref, bf16[1024,256]{1,0:T(8,128)(2,1)} %copy-done.15, bf16[1024,256]{1,0:T(8,128)(2,1)} %copy-done.17), custom_call_target="tpu_custom_call" | custom-call | flops 21474836480 | bytes 9437184 | tf_op jit(solution)/shard_map/attend/pallas_call | solution.py:73
  143.1 23.6 %fusion.71 = f32[1024,4096]{1,0:T(8,128)} fusion(bf16[1024,2048]{1,0:T(8,128)(2,1)} %attend.2, bf16[2048,4096]{1,0:T(8,128)(2,1)} %bitcast.126), kind=kOutput, calls=%fused_computation.73 | convolution fusion | flops 17179869184 | bytes 37748736 | tf_op jit(solution)/shard_map/dot_general | solution.py:139
  172.9 22.4 %fusion.36.q_ref = bf16[1024,2048]{1,0:T(8,128)(2,1)} fusion(bf16[512,8,16,128]{3,2,1,0:T(8,128)(2,1)} %bitcast.125, bf16[1,1024,4096]{2,1,0:T(8,128)(2,1)S(1)} %copy-done.10), kind=kOutput, calls=%fused_computation.38 | convolution fusion | flops 17181966336 | bytes 29360128 | tf_op jit(solution)/shard_map/dot_general | solution.py:137
  196.1 41.1 %attend.3 = bf16[1024,2048]{1,0:T(8,128)(2,1)} custom-call(s32[1]{0:T(128)} %bitcast.1.cp_ref, bf16[1024,2048]{1,0:T(8,128)(2,1)} %fusion.36.q_ref, bf16[1024,256]{1,0:T(8,128)(2,1)} %copy-done.14, bf16[1024,256]{1,0:T(8,128)(2,1)} %copy-done.16), custom_call_target="tpu_custom_call" | custom-call | flops 21474836480 | bytes 9437184 | tf_op jit(solution)/shard_map/attend/pallas_call | solution.py:73
  237.3 23.6 %fusion.72 = f32[1024,4096]{1,0:T(8,128)} fusion(bf16[1024,2048]{1,0:T(8,128)(2,1)} %attend.3, bf16[2048,4096]{1,0:T(8,128)(2,1)} %bitcast.127), kind=kOutput, calls=%fused_computation.74 | convolution fusion | flops 17179869184 | bytes 37748736 | tf_op jit(solution)/shard_map/dot_general | solution.py:139
  261.0 23.7 %reduce-scatter.3.cloned.1.call-done = f32[256,4096]{1,0:T(8,128)} async-done(((f32[1024,4096]{1,0:T(8,128)}), f32[256,4096]{1,0:T(8,128)}) %reduce-scatter.3.cloned.1.call-update) | async-done | bytes 4194320 | tf_op jit(solution)/shard_map/reduce_scatter | solution.py:140
  289.5 116.4 %reduce-scatter.5.cloned.1.call-done = f32[256,4096]{1,0:T(8,128)} async-done(((f32[1024,4096]{1,0:T(8,128)}), f32[256,4096]{1,0:T(8,128)}) %reduce-scatter.5.cloned.1.call-update) | async-done | bytes 4194320 | tf_op jit(solution)/shard_map/reduce_scatter | solution.py:140
  410.6 83.6 %all-gather.16.cloned.1.call-done = bf16[2048,4096]{1,0:T(8,128)(2,1)} async-done(((bf16[256,4096]{1,0:T(8,128)(2,1)}), bf16[2048,4096]{1,0:T(8,128)(2,1)}) %all-gather.16.cloned.1.call-update) | async-done | bytes 16777232 | tf_op jit(solution)/shard_map/all_gather | solution.py:144
  494.2 11.5 %convolution_convert_fusion = bf16[8,128,4096]{2,1,0:T(8,128)(2,1)} fusion(bf16[8,256,4096]{2,1,0:T(8,128)(2,1)} %bitcast.112, bf16[8,2,128,256]{3,2,0,1:T(8,128)(2,1)S(1)} %copy-done.5), kind=kOutput, calls=%fused_computation.21 | convolution fusion | flops 2151677952 | bytes 25690112 | tf_op jit(solution)/shard_map/dst,dth->dsh/dot_general | solution.py:145
  505.8 21.0 %fusion.10 = f32[1024,1536]{1,0:T(8,128)} fusion(bf16[1024,4096]{1,0:T(8,128)(2,1)} %bitcast.115, bf16[1,4096,1536]{2,1,0:T(8,128)(2,1)} %param.18), kind=kOutput, calls=%fused_computation.10 | convolution fusion | flops 12884901888 | bytes 27262976 | tf_op jit(solution)/shard_map/dot_general | solution.py:148
  526.8 16.1 %multiply_convert_fusion = bf16[1024,1536]{1,0:T(8,128)(2,1)S(1)} fusion(f32[1024,1536]{1,0:T(8,128)} %fusion.10, bf16[1024,4096]{1,0:T(8,128)(2,1)S(1)} %bitcast.116, bf16[1,4096,1536]{2,1,0:T(8,128)(2,1)S(1)} %bitcast.129), kind=kOutput, calls=%fused_computation.25 | convolution fusion | flops 12894339072 | bytes 30408704 | tf_op jit(solution)/shard_map/dot_general | solution.py:147
  542.9 18.2 %fusion.24 = bf16[1024,4096]{1,0:T(8,128)(2,1)} fusion(bf16[1024,1536]{1,0:T(8,128)(2,1)S(1)} %multiply_convert_fusion, bf16[1,1536,4096]{2,1,0:T(8,128)(2,1)} %param.19), kind=kOutput, calls=%fused_computation.24 | convolution fusion | flops 12889096192 | bytes 24117248 | tf_op jit(solution)/shard_map/dot_general | solution.py:150
  565.0 25.0 %all-gather.12.cloned.1.call-done = bf16[2048,4096]{1,0:T(8,128)(2,1)} async-done(((bf16[256,4096]{1,0:T(8,128)(2,1)}), bf16[2048,4096]{1,0:T(8,128)(2,1)}) %all-gather.12.cloned.1.call-update) | async-done | bytes 16777232 | tf_op jit(solution)/shard_map/all_gather | solution.py:144
  590.0 11.5 %convolution_convert_fusion.1 = bf16[8,128,4096]{2,1,0:T(8,128)(2,1)} fusion(bf16[8,256,4096]{2,1,0:T(8,128)(2,1)} %bitcast.111, bf16[8,2,128,256]{3,2,0,1:T(8,128)(2,1)S(1)} %copy-done.5), kind=kOutput, calls=%fused_computation.22 | convolution fusion | flops 2151677952 | bytes 25690112 | tf_op jit(solution)/shard_map/dst,dth->dsh/dot_general | solution.py:145
  601.5 19.6 %fusion.12 = f32[1024,1536]{1,0:T(8,128)} fusion(bf16[1024,4096]{1,0:T(8,128)(2,1)} %bitcast.113, bf16[1,4096,1536]{2,1,0:T(8,128)(2,1)} %param.18), kind=kOutput, calls=%fused_computation.12 | convolution fusion | flops 12884901888 | bytes 27262976 | tf_op jit(solution)/shard_map/dot_general | solution.py:148
  621.2 16.1 %multiply_convert_fusion.1 = bf16[1024,1536]{1,0:T(8,128)(2,1)S(1)} fusion(f32[1024,1536]{1,0:T(8,128)} %fusion.12, bf16[1024,4096]{1,0:T(8,128)(2,1)S(1)} %bitcast.114, bf16[1,4096,1536]{2,1,0:T(8,128)(2,1)S(1)} %bitcast.131), kind=kOutput, calls=%fused_computation.26 | convolution fusion | flops 12894339072 | bytes 30408704 | tf_op jit(solution)/shard_map/dot_general | solution.py:147
  637.3 18.4 %fusion.21 = bf16[1024,4096]{1,0:T(8,128)(2,1)} fusion(bf16[1024,1536]{1,0:T(8,128)(2,1)S(1)} %multiply_convert_fusion.1, bf16[1,1536,4096]{2,1,0:T(8,128)(2,1)} %param.19), kind=kOutput, calls=%fused_computation.23 | convolution fusion | flops 12889096192 | bytes 24117248 | tf_op jit(solution)/shard_map/dot_general | solution.py:150
  655.8 12.8 %all-to-all-done.1 = bf16[8,128,4096]{2,1,0:T(8,128)(2,1)} async-done(((bf16[8,128,4096]{2,1,0:T(8,128)(2,1)}), bf16[8,128,4096]{2,1,0:T(8,128)(2,1)}, u32[]{:S(2)}, u32[]{:S(2)}) %all-to-all-start.1) | async-done | bytes 8388640 | tf_op jit(solution)/shard_map/all_to_all | solution.py:151
  668.6 11.3 %all-to-all-start = ((bf16[8,128,4096]{2,1,0:T(8,128)(2,1)}), bf16[8,128,4096]{2,1,0:T(8,128)(2,1)}, u32[]{:S(2)}, u32[]{:S(2)}) async-start(bf16[8,128,4096]{2,1,0:T(8,128)(2,1)} %bitcast.118), calls=%async_computation.1 | async-start | bytes 16777216 | tf_op jit(solution)/shard_map/all_to_all | solution.py:151
  680.0 9.4 %convolution_convert_fusion.2 = bf16[512,4096]{1,0:T(8,128)(2,1)} fusion(bf16[1024,4096]{1,0:T(8,128)(2,1)} %bitcast.30, bf16[2,512,1024]{2,1,0:T(8,128)(2,1)S(1)} %copy-done.7), kind=kOutput, calls=%fused_computation.27 | convolution fusion | flops 4297064448 | bytes 13631488 | tf_op jit(solution)/shard_map/dot_general | solution.py:153
  689.4 85.5 %all-to-all-done = bf16[8,128,4096]{2,1,0:T(8,128)(2,1)} async-done(((bf16[8,128,4096]{2,1,0:T(8,128)(2,1)}), bf16[8,128,4096]{2,1,0:T(8,128)(2,1)}, u32[]{:S(2)}, u32[]{:S(2)}) %all-to-all-start) | async-done | bytes 8388640 | tf_op jit(solution)/shard_map/all_to_all | solution.py:151
  (88 shorter events, 52.3 us)
Async XLA Ops:
  6.5 64.3 %all-gather.10.cloned.1.call-start = ((), (), s32[]{:S(2)}) async-start(), calls=%async_computation.6 | async-start | bytes 10485760 | tf_op jit(solution)/shard_map/all_gather | solution.py:132
  12.0 58.9 %copy-start.12 = (bf16[4096,1,128]{2,0,1:T(8,128)(2,1)S(1)}, bf16[4096,1,128]{2,0,1:T(8,128)(2,1)}, u32[]{:S(2)}) copy-start(bf16[4096,1,128]{2,0,1:T(8,128)(2,1)} %param.15) | copy-start | bytes 3145732
  12.0 58.9 %copy-start.13 = (bf16[4096,1,128]{2,0,1:T(8,128)(2,1)S(1)}, bf16[4096,1,128]{2,0,1:T(8,128)(2,1)}, u32[]{:S(2)}) copy-start(bf16[4096,1,128]{2,0,1:T(8,128)(2,1)} %param.14) | copy-start | bytes 3145732
  12.0 154.7 %all-gather.14.cloned.1.call-start = ((), (), s32[]{:S(2)}) async-start(), calls=%async_computation.8 | async-start | bytes 10485760 | tf_op jit(solution)/shard_map/all_gather | solution.py:132
  12.8 271.9 %reduce-scatter.3.cloned.1.call-start = ((), (), s32[]{:S(2)}) async-start(), calls=%async_computation.4 | async-start | bytes 20971520 | tf_op jit(solution)/shard_map/reduce_scatter | solution.py:140
  76.7 24.4 %copy-start.15 = (bf16[1024,256]{1,0:T(8,128)(2,1)}, bf16[1024,256]{1,0:T(8,128)(2,1)S(1)}, u32[]{:S(2)}) copy-start(bf16[1024,256]{1,0:T(8,128)(2,1)S(1)} %fusion.45.own_ref) | copy-start | bytes 1572868
  76.7 24.4 %collective-permute-start = (bf16[1024,256]{1,0:T(8,128)(2,1)S(1)}, bf16[1024,256]{1,0:T(8,128)(2,1)S(1)}, u32[]{:S(2)}, u32[]{:S(2)}) collective-permute-start(bf16[1024,256]{1,0:T(8,128)(2,1)S(1)} %fusion.45.own_ref), channel_id=1, source_target_pairs={{0,4},{4,0},{1,5},{5,1},{2,6},{6,2},{3,7},{7,3}} | collective-permute-start | bytes 1572872 | tf_op jit(solution)/shard_map/ppermute | solution.py:136
  166.7 239.2 %reduce-scatter.5.cloned.1.call-start = ((), (), s32[]{:S(2)}) async-start(), calls=%async_computation.5 | async-start | bytes 20971520 | tf_op jit(solution)/shard_map/reduce_scatter | solution.py:140
  172.6 22.7 %copy-start.14 = (bf16[1024,256]{1,0:T(8,128)(2,1)}, bf16[1024,256]{1,0:T(8,128)(2,1)S(1)}, u32[]{:S(2)}) copy-start(bf16[1024,256]{1,0:T(8,128)(2,1)S(1)} %fusion.49.own_ref) | copy-start | bytes 1572868
  172.6 22.7 %collective-permute-start.1 = (bf16[1024,256]{1,0:T(8,128)(2,1)S(1)}, bf16[1024,256]{1,0:T(8,128)(2,1)S(1)}, u32[]{:S(2)}, u32[]{:S(2)}) collective-permute-start(bf16[1024,256]{1,0:T(8,128)(2,1)S(1)} %fusion.49.own_ref), channel_id=1, source_target_pairs={{0,4},{4,0},{1,5},{5,1},{2,6},{6,2},{3,7},{7,3}} | collective-permute-start | bytes 1572872 | tf_op jit(solution)/shard_map/ppermute | solution.py:136
  260.9 144.9 %copy-start.4 = (bf16[256,4096]{1,0:T(8,128)(2,1)S(1)}, bf16[256,4096]{1,0:T(8,128)(2,1)}, u32[]{:S(2)}) copy-start(bf16[256,4096]{1,0:T(8,128)(2,1)} %get-tuple-element.12) | copy-start | bytes 6291460
  260.9 233.3 %all-gather.16.cloned.1.call-start = ((), (), s32[]{:S(2)}) async-start(), calls=%async_computation.9 | async-start | bytes 18874368 | tf_op jit(solution)/shard_map/all_gather | solution.py:144
  289.5 204.7 %copy-start.5 = (bf16[8,2,128,256]{3,2,0,1:T(8,128)(2,1)S(1)}, bf16[8,2,128,256]{3,2,0,1:T(8,128)(2,1)}, u32[]{:S(2)}) copy-start(bf16[8,2,128,256]{3,2,0,1:T(8,128)(2,1)} %fusion.43) | copy-start | bytes 3145732
  410.0 180.0 %all-gather.12.cloned.1.call-start = ((), (), s32[]{:S(2)}) async-start(), calls=%async_computation.7 | async-start | bytes 18874368 | tf_op jit(solution)/shard_map/all_gather | solution.py:144
  494.2 32.6 %slice-start = ((s8[12582912]{0:T(1024)(128)(4,1)}), s8[4194304]{0:T(1024)(128)(4,1)S(1)}, s32[]{:S(2)}) async-start(s8[12582912]{0:T(1024)(128)(4,1)} %bitcast.128), calls=%async_computation.10 | async-start | bytes 8388608
  505.8 21.1 %copy-start.3 = (bf16[8,128,4096]{2,1,0:T(8,128)(2,1)S(1)}, bf16[8,128,4096]{2,1,0:T(8,128)(2,1)}, u32[]{:S(2)}) copy-start(bf16[8,128,4096]{2,1,0:T(8,128)(2,1)} %convolution_convert_fusion) | copy-start | bytes 25165828
  505.8 21.1 %slice-start.1 = ((s8[12582912]{0:T(1024)(128)(4,1)}), s8[4194304]{0:T(1024)(128)(4,1)S(1)}, s32[]{:S(2)}) async-start(s8[12582912]{0:T(1024)(128)(4,1)} %bitcast.128), calls=%async_computation.11 | async-start | bytes 8388608
  505.8 21.1 %slice-start.2 = ((s8[12582912]{0:T(1024)(128)(4,1)}), s8[4194304]{0:T(1024)(128)(4,1)S(1)}, s32[]{:S(2)}) async-start(s8[12582912]{0:T(1024)(128)(4,1)} %bitcast.128), calls=%async_computation.12 | async-start | bytes 8388608
  561.1 107.5 %all-to-all-start.1 = ((bf16[8,128,4096]{2,1,0:T(8,128)(2,1)}), bf16[8,128,4096]{2,1,0:T(8,128)(2,1)}, u32[]{:S(2)}, u32[]{:S(2)}) async-start(bf16[8,128,4096]{2,1,0:T(8,128)(2,1)} %bitcast.117), calls=%async_computation.3 | async-start | bytes 16777216 | tf_op jit(solution)/shard_map/all_to_all | solution.py:151
  590.0 31.2 %slice-start.3 = ((s8[12582912]{0:T(1024)(128)(4,1)}), s8[4194304]{0:T(1024)(128)(4,1)S(1)}, s32[]{:S(2)}) async-start(s8[12582912]{0:T(1024)(128)(4,1)} %bitcast.130), calls=%async_computation.13 | async-start | bytes 8388608
  601.5 19.7 %copy-start.2 = (bf16[8,128,4096]{2,1,0:T(8,128)(2,1)S(1)}, bf16[8,128,4096]{2,1,0:T(8,128)(2,1)}, u32[]{:S(2)}) copy-start(bf16[8,128,4096]{2,1,0:T(8,128)(2,1)} %convolution_convert_fusion.1) | copy-start | bytes 25165828
  601.5 19.7 %slice-start.4 = ((s8[12582912]{0:T(1024)(128)(4,1)}), s8[4194304]{0:T(1024)(128)(4,1)S(1)}, s32[]{:S(2)}) async-start(s8[12582912]{0:T(1024)(128)(4,1)} %bitcast.130), calls=%async_computation.14 | async-start | bytes 8388608
  601.5 19.7 %slice-start.5 = ((s8[12582912]{0:T(1024)(128)(4,1)}), s8[4194304]{0:T(1024)(128)(4,1)S(1)}, s32[]{:S(2)}) async-start(s8[12582912]{0:T(1024)(128)(4,1)} %bitcast.130), calls=%async_computation.15 | async-start | bytes 8388608
  668.6 106.3 %all-to-all-start = ((bf16[8,128,4096]{2,1,0:T(8,128)(2,1)}), bf16[8,128,4096]{2,1,0:T(8,128)(2,1)}, u32[]{:S(2)}, u32[]{:S(2)}) async-start(bf16[8,128,4096]{2,1,0:T(8,128)(2,1)} %bitcast.118), calls=%async_computation.1 | async-start | bytes 16777216 | tf_op jit(solution)/shard_map/all_to_all | solution.py:151
  (10 other events, 62.3 us)
Sparse Core Ops, SparseCore 0:
  12.1 58.6 all-gather.9
  72.4 55.7 all-gather.13
  166.8 117.8 reduce-scatter.2
  287.1 118.7 reduce-scatter.4
  410.1 84.0 all-gather.15
  495.9 94.0 all-gather.11
